TPU v7x, 32 devices: a whole 2x2x4 slice. The times are simulated.
32 devices in a mesh: grp: 4 (over z), dp: 2 (over x), tp: 4 (over y, core).
Axes of the slice: x: 2, y: 2, z: 4, core: 2. Of those that a mesh axis runs over, the one named last changes fastest.
Arguments:
- hidden_last: bfloat16 [128, 5120], P(('grp', 'dp')), may hold values from -6 to 6
- gain: float32 [5120], replicated, may hold values from 0.25 to 1.75
- w_query: bfloat16 [5120, 2560], P('dp', 'tp'), may hold values from -0.078125 to 0.078125
- w_key: bfloat16 [5120, 512], P('dp', 'tp'), may hold values from -0.078125 to 0.078125
- w_value: bfloat16 [5120, 512], P('dp', 'tp'), may hold values from -0.078125 to 0.078125
- w_out: bfloat16 [2560, 5120], P('tp'), may hold values from -0.125 to 0.125
- cache_keys: bfloat16 [128, 128, 512], P(('grp', 'dp'), None, 'tp'), may hold values from -6 to 6
- cache_values: bfloat16 [128, 128, 512], P(('grp', 'dp'), None, 'tp'), may hold values from -6 to 6
- cache_lengths: int32 [128], P(('grp', 'dp')), may hold values from 1 to 128
- reward_vec: float32 [5120], replicated, may hold values from -0.078125 to 0.078125
- response_counts: int32 [128], P('grp'), may hold values from 4 to 16
- assignment: int32 [128], P('grp'), may hold values from 0 to 1, as said below
- responses: bfloat16 [128, 16, 5120], P(('grp', 'dp'), None, 'tp'), may hold values from -6 to 6
- cotangent: bfloat16 [128, 16, 5120], P(('grp', 'dp'), None, 'tp'), may hold values from -6 to 6
Outputs:
- decoded: bfloat16 [128, 5120], P(('grp', 'dp'))
- advantage: float32 [128], P(('grp', 'dp'))
- layer_out: bfloat16 [128, 16, 5120], P(('grp', 'dp'), None, 'tp')
- grad_query: float32 [5120, 2560], P('dp', 'tp')
- grad_key: float32 [5120, 512], P('dp', 'tp')
- grad_value: float32 [5120, 512], P('dp', 'tp')
Inputs may be any that keep to these rules, and one draw needn't show every extreme that they name: `assignment`: within each group, every training shard receives exactly 16 rows, and from the 16 rows of one device at most 10 rows go to one training shard; that most is reached for some shard in every group.
All inputs are finite; a program needn't handle non-finite values.
Results may differ from a plain program's by a relative error of at most 0.025.
Values may be sent and summed in bfloat16 or wider, within the bound.
A program may use at most 128 MiB of HBM per device.

v0:
```python
import jax
import jax.numpy as jnp
from jax import lax
from jax.sharding import PartitionSpec as P

HEAD_DIM = 128
STEPS = 2


def norm_rows(values, gain):
    wide = values.astype(jnp.float32)
    meansq = jnp.mean(wide * wide, axis=-1, keepdims=True)
    return (wide * lax.rsqrt(meansq + 1e-06) * gain).astype(jnp.bfloat16)


def rounded(values):
    return lax.optimization_barrier(values.astype(jnp.bfloat16)).astype(jnp.float32)


def decode_attend(query, cache_k, cache_v, lengths, new_k, new_v):
    rows_n = query.shape[0]
    slots = cache_k.shape[1]
    kv_n = cache_k.shape[2] // HEAD_DIM
    per_kv = query.shape[1] // cache_k.shape[2]
    scale = 1.0 / HEAD_DIM**0.5
    quer = query.reshape(rows_n, kv_n, per_kv, HEAD_DIM)
    keys_c = cache_k.reshape(rows_n, slots, kv_n, HEAD_DIM)
    vals_c = cache_v.reshape(rows_n, slots, kv_n, HEAD_DIM)
    keys_n = new_k.reshape(rows_n, -1, kv_n, HEAD_DIM)
    vals_n = new_v.reshape(rows_n, -1, kv_n, HEAD_DIM)
    score_c = (
        jnp.einsum("rkgd,rckd->rkgc", quer, keys_c, preferred_element_type=jnp.float32) * scale
    )
    score_n = (
        jnp.einsum("rkgd,rnkd->rkgn", quer, keys_n, preferred_element_type=jnp.float32) * scale
    )
    live = (jnp.arange(slots, dtype=jnp.int32)[None, :] < lengths[:, None])[:, None, None, :]
    score_c = jnp.where(live, score_c, -1e30)
    scores = jnp.concatenate([score_c, score_n], axis=-1)
    expo = jnp.exp(scores)
    weights = (expo / jnp.sum(expo, axis=-1, keepdims=True)).astype(jnp.bfloat16)
    context = jnp.einsum(
        "rkgc,rckd->rkgd", weights[..., :slots], vals_c, preferred_element_type=jnp.float32
    )
    context = context + jnp.einsum(
        "rkgn,rnkd->rkgd", weights[..., slots:], vals_n, preferred_element_type=jnp.float32
    )
    return context.reshape(rows_n, -1).astype(jnp.bfloat16)


def attend(query, keys, values, counts):
    rows_n = counts.shape[0]
    tokens = query.shape[0]
    length = tokens // rows_n
    kv_n = keys.shape[1] // HEAD_DIM
    per_kv = query.shape[1] // keys.shape[1]
    scale = 1.0 / HEAD_DIM**0.5
    quer = query.reshape(rows_n, length, kv_n, per_kv, HEAD_DIM).astype(jnp.float32)
    keyf = keys.reshape(rows_n, length, kv_n, HEAD_DIM).astype(jnp.float32)
    valf = values.reshape(rows_n, length, kv_n, HEAD_DIM).astype(jnp.float32)
    scores = jnp.einsum("rikgd,rjkd->rkgij", quer, keyf) * scale
    slot = jnp.arange(length, dtype=jnp.int32)
    causal = (slot[None, :] <= slot[:, None])[None, :, :]
    inside = slot[None, None, :] < counts[:, None, None]
    mask = (causal & inside)[:, None, None, :, :]
    scores = jnp.where(mask, scores, -1e30)
    expo = jnp.exp(scores)
    weights = (
        (expo / jnp.sum(expo, axis=-1, keepdims=True)).astype(jnp.bfloat16).astype(jnp.float32)
    )
    context = jnp.einsum("rkgij,rjkd->rikgd", weights, valf)
    return context.reshape(tokens, -1).astype(jnp.bfloat16)


def slot_valid(counts, length):
    slot = jnp.arange(length, dtype=jnp.int32)
    return (slot[None, :] < counts[:, None]).reshape(-1)


def exclusive_rank(labels, classes):
    onehot = (labels[:, None] == jnp.arange(classes, dtype=jnp.int32)[None, :]).astype(jnp.int32)
    return jnp.sum((jnp.cumsum(onehot, axis=0) - onehot) * onehot, axis=1)


def on_device(
    hidden_last,
    gain,
    w_query,
    w_key,
    w_value,
    w_out,
    cache_keys,
    cache_values,
    cache_lengths,
    reward_vec,
    response_counts,
    assignment,
    responses,
    cotangent,
):
    query_full, key_full, value_full = (
        lax.all_gather(w_query, "dp", axis=0, tiled=True),
        lax.all_gather(w_key, "dp", axis=0, tiled=True),
        lax.all_gather(w_value, "dp", axis=0, tiled=True),
    )
    state = hidden_last
    keys_new = []
    values_new = []
    for step in range(STEPS):
        normed = norm_rows(state, gain)
        query = jnp.dot(normed, query_full, preferred_element_type=jnp.float32).astype(jnp.bfloat16)
        keys_new.append(
            jnp.dot(normed, key_full, preferred_element_type=jnp.float32).astype(jnp.bfloat16)
        )
        values_new.append(
            jnp.dot(normed, value_full, preferred_element_type=jnp.float32).astype(jnp.bfloat16)
        )
        context = decode_attend(
            query,
            cache_keys,
            cache_values,
            cache_lengths,
            jnp.stack(keys_new, 1),
            jnp.stack(values_new, 1),
        )
        partial_out = jnp.dot(context, w_out, preferred_element_type=jnp.float32)
        state = (
            state.astype(jnp.float32)
            + lax.psum(partial_out.astype(jnp.bfloat16), "tp").astype(jnp.float32)
        ).astype(jnp.bfloat16)
    reward = jnp.sum(state.astype(jnp.float32) * reward_vec, axis=-1)
    total, squares = lax.psum((jnp.sum(reward), jnp.sum(reward * reward)), "dp")
    shards = lax.axis_size("dp")
    rows_dev = reward.shape[0]
    members = rows_dev * shards
    mean = total / members
    spread = squares / members - mean * mean
    advantage = (reward - mean) / jnp.sqrt(spread + 1e-05)
    adv_short = advantage.astype(jnp.bfloat16)
    myself = lax.axis_index("dp")
    group_rows = assignment.shape[0]
    positions = jnp.arange(group_rows, dtype=jnp.int32)
    owner_rank = exclusive_rank(assignment, shards)
    wanted = (assignment[None, :] == myself) & (
        owner_rank[None, :] == jnp.arange(rows_dev, dtype=jnp.int32)[:, None]
    )
    chosen = jnp.sum(jnp.where(wanted, positions[None, :], 0), axis=1)
    every_row, every_adv = (
        lax.all_gather(responses, "dp", axis=0, tiled=True),
        lax.all_gather(adv_short, "dp", axis=0, tiled=True),
    )
    mine = jnp.take(every_row, chosen, axis=0)
    my_adv = jnp.take(every_adv, chosen)
    length = mine.shape[1]
    tokens = mine.shape[0] * length
    local_in = mine.reshape(tokens, -1)
    local_cot = cotangent.reshape(tokens, -1)
    full_in, full_cot = (
        lax.all_gather(local_in, "tp", axis=1, tiled=True),
        lax.all_gather(local_cot, "tp", axis=1, tiled=True),
    )
    normed = norm_rows(full_in, gain)
    query = jnp.dot(normed, query_full, preferred_element_type=jnp.float32).astype(jnp.bfloat16)
    keys = jnp.dot(normed, key_full, preferred_element_type=jnp.float32).astype(jnp.bfloat16)
    values = jnp.dot(normed, value_full, preferred_element_type=jnp.float32).astype(jnp.bfloat16)
    counts = jnp.take(response_counts, chosen)
    valid = slot_valid(counts, length)
    context, pull = jax.vjp(lambda a, b, c: attend(a, b, c, counts), query, keys, values)
    partial_out = jnp.dot(context, w_out, preferred_element_type=jnp.float32)
    layer = (
        local_in.astype(jnp.float32)
        + lax.psum_scatter(
            partial_out.astype(jnp.bfloat16), "tp", scatter_dimension=1, tiled=True
        ).astype(jnp.float32)
    ).astype(jnp.bfloat16)
    token_weight = jnp.repeat(my_adv.astype(jnp.float32), length) * valid.astype(jnp.float32)
    upstream = (token_weight[:, None] * full_cot.astype(jnp.float32)).astype(jnp.bfloat16)
    d_context = lax.dot_general(
        upstream, w_out, (((1,), (1,)), ((), ())), preferred_element_type=jnp.float32
    ).astype(jnp.bfloat16)
    d_query, d_key, d_value = pull(d_context)
    block_rows = lax.all_to_all(normed, "dp", split_axis=1, concat_axis=0, tiled=True)
    width = block_rows.shape[1]
    empty_q = jnp.zeros((width, d_query.shape[1]), jnp.float32)
    empty_k = jnp.zeros((width, d_key.shape[1]), jnp.float32)
    empty_v = jnp.zeros((width, d_value.shape[1]), jnp.float32)
    pieces = (
        lax.all_gather(d_query, "dp", axis=0, tiled=True),
        lax.all_gather(d_key, "dp", axis=0, tiled=True),
        lax.all_gather(d_value, "dp", axis=0, tiled=True),
    )
    span = pieces[0].shape[0]
    count = span // tokens
    totals = list((empty_q, empty_k, empty_v))
    for member in range(count):
        left = block_rows[member * tokens : (member + 1) * tokens]
        for which in range(3):
            right = pieces[which][member * tokens : (member + 1) * tokens]
            term = lax.dot_general(
                left, right, (((0,), (0,)), ((), ())), preferred_element_type=jnp.float32
            )
            totals[which] = totals[which] + rounded(term)
    shard_q, shard_k, shard_v = tuple(totals)
    grad_q, grad_k, grad_v = (
        lax.psum(shard_q.astype(jnp.bfloat16), "grp").astype(jnp.float32),
        lax.psum(shard_k.astype(jnp.bfloat16), "grp").astype(jnp.float32),
        lax.psum(shard_v.astype(jnp.bfloat16), "grp").astype(jnp.float32),
    )
    return (state, advantage, layer.reshape(mine.shape[0], length, -1), grad_q, grad_k, grad_v)


def solution(mesh):
    return jax.shard_map(
        on_device,
        mesh=mesh,
        in_specs=(
            P(("grp", "dp"), None),
            P(),
            P("dp", "tp"),
            P("dp", "tp"),
            P("dp", "tp"),
            P("tp", None),
            P(("grp", "dp"), None, "tp"),
            P(("grp", "dp"), None, "tp"),
            P(("grp", "dp")),
            P(),
            P("grp"),
            P("grp"),
            P(("grp", "dp"), None, "tp"),
            P(("grp", "dp"), None, "tp"),
        ),
        out_specs=(
            P(("grp", "dp"), None),
            P(("grp", "dp")),
            P(("grp", "dp"), None, "tp"),
            P("dp", "tp"),
            P("dp", "tp"),
            P("dp", "tp"),
        ),
        check_vma=False,
    )
```

profile of v0, /device:TPU:0, one launch (start us, length us, event | category | flops | bytes accessed | tf_op | source)
XLA Modules:
  0.0 569.9 jit_solution(5665463674847834380)
XLA Ops:
  9.7 26.9 %all-gather.9.cloned.1.call-done = bf16[5120,128]{1,0:T(8,128)(2,1)} async-done(((bf16[2560,128]{1,0:T(8,128)(2,1)}), bf16[5120,128]{1,0:T(8,128)(2,1)}) %all-gather.9.cloned.1.call-update) | async-done | bytes 1310736 | tf_op jit(solution)/shard_map/all_gather | solution.py:103
  36.6 1.6 convolution_convert_fusion.20
  38.2 24.2 %all-gather.11.cloned.1.call-done = bf16[5120,128]{1,0:T(8,128)(2,1)} async-done(((bf16[2560,128]{1,0:T(8,128)(2,1)}), bf16[5120,128]{1,0:T(8,128)(2,1)}) %all-gather.11.cloned.1.call-update) | async-done | bytes 1310736 | tf_op jit(solution)/shard_map/all_gather | solution.py:104
  64.0 83.2 %all-gather.7.cloned.1.call-done = bf16[5120,640]{1,0:T(8,128)(2,1)} async-done(((bf16[2560,640]{1,0:T(8,128)(2,1)}), bf16[5120,640]{1,0:T(8,128)(2,1)}) %all-gather.7.cloned.1.call-update) | async-done | bytes 6553616 | tf_op jit(solution)/shard_map/all_gather | solution.py:102
  147.2 3.8 convolution_convert_fusion.16
  152.7 4.5 convolution_convert_fusion.2
  159.6 29.7 %all-reduce.7.cloned.1.call-done = bf16[16,5120]{1,0:T(8,128)(2,1)} async-done(((bf16[16,5120]{1,0:T(8,128)(2,1)}), bf16[16,5120]{1,0:T(8,128)(2,1)}) %all-reduce.7.cloned.1.call-update) | async-done | bytes 163856 | tf_op jit(solution)/shard_map/psum | solution.py:129
  191.4 4.5 convolution_convert_fusion.15
  200.7 4.5 convolution_convert_fusion.1
  205.3 9.6 %all-gather.13.cloned.1.call-done = bf16[32,16,1280]{2,1,0:T(8,128)(2,1)} async-done(((bf16[16,16,1280]{2,1,0:T(8,128)(2,1)}), bf16[32,16,1280]{2,1,0:T(8,128)(2,1)}) %all-gather.13.cloned.1.call-update) | async-done | bytes 1310736 | tf_op jit(solution)/shard_map/all_gather | solution.py:149
  215.0 1.9 gather_fusion
  216.9 32.8 %all-reduce.9.cloned.1.call-done = bf16[16,5120]{1,0:T(8,128)(2,1)} async-done(((bf16[16,5120]{1,0:T(8,128)(2,1)}), bf16[16,5120]{1,0:T(8,128)(2,1)}) %all-reduce.9.cloned.1.call-update) | async-done | bytes 163856 | tf_op jit(solution)/shard_map/psum | solution.py:129
  249.7 2.3 fusion.36
  252.5 5.5 all-reduce.1
  261.4 4.9 all-reduce
  270.2 23.7 %all-gather.15.cloned.1.call-done = bf16[256,5120]{1,0:T(8,128)(2,1)} async-done(((bf16[256,1280]{1,0:T(8,128)(2,1)}), bf16[256,5120]{1,0:T(8,128)(2,1)}) %all-gather.15.cloned.1.call-update) | async-done | bytes 2621456 | tf_op jit(solution)/shard_map/all_gather | solution.py:159
  293.9 2.5 fusion
  297.2 5.1 convolution_convert_fusion.11
  302.7 2.7 convolution_convert_fusion.13
  307.5 6.6 %convolution_convert_fusion = bf16[256,5120]{1,0:T(8,128)(2,1)} fusion(bf16[640,5120]{1,0:T(8,128)(2,1)} %param.19, bf16[32,8,5,128]{3,2,1,0:T(8,128)(2,1)S(1)} %bitcast.188), kind=kOutput, calls=%fused_computation.6 | convolution fusion | flops 1679032320 | bytes 9502720 | tf_op jit(solution)/shard_map/dot_general | solution.py:169
  314.2 6.9 %all-gather.17.cloned.1.call-done = bf16[256,5120]{1,0:T(8,128)(2,1)} async-done(((bf16[256,1280]{1,0:T(8,128)(2,1)}), bf16[256,5120]{1,0:T(8,128)(2,1)}) %all-gather.17.cloned.1.call-update) | async-done | bytes 2621456 | tf_op jit(solution)/shard_map/all_gather | solution.py:160
  321.0 5.9 %fusion.6 = bf16[256,640]{1,0:T(8,128)(2,1)S(1)} fusion(bf16[640,5120]{1,0:T(8,128)(2,1)} %param.19, bf16[256,5120]{1,0:T(8,128)(2,1)} %all-gather.17.cloned.1.call-done, f32[256]{0:T(256)S(1)} %mul.176), kind=kOutput, calls=%fused_computation.29 | convolution fusion | flops 1681817600 | bytes 9503744 | tf_op jit(solution)/shard_map/dot_general | solution.py:178
  327.3 1.7 copy.184
  329.0 4.2 all-to-all-start
  333.5 1.9 fusion.21
  337.6 28.2 %all_gather.38 = bf16[512,128]{1,0:T(8,128)(2,1)S(1)} all-gather(bf16[256,128]{1,0:T(8,128)(2,1)S(1)} %bitcast.195), channel_id=1, replica_groups=mesh['grp'=4,'dp'=2,'tp'=4] {'dp'}, dimensions={0}, use_global_device_ids=true | all-gather | bytes 196608 | tf_op jit(solution)/shard_map/all_gather | solution.py:189
  366.1 4.9 all_gather.39
  371.0 8.6 %all_gather.37 = bf16[512,640]{1,0:T(8,128)(2,1)} all-gather(bf16[256,640]{1,0:T(8,128)(2,1)S(1)} %bitcast.185), channel_id=1, replica_groups=mesh['grp'=4,'dp'=2,'tp'=4] {'dp'}, dimensions={0}, use_global_device_ids=true | all-gather | bytes 983040 | tf_op jit(solution)/shard_map/all_gather | solution.py:188
  385.8 2.6 add_convert_fusion
  389.5 2.2 add_convert_fusion.3
  391.7 163.8 %all-reduce.11.cloned.1.call-done = (bf16[2560,640]{1,0:T(8,128)(2,1)}, bf16[2560,128]{1,0:T(8,128)(2,1)}, bf16[2560,128]{1,0:T(8,128)(2,1)}) async-done(((bf16[2560,640]{1,0:T(8,128)(2,1)}, bf16[2560,128]{1,0:T(8,128)(2,1)}, bf16[2560,128]{1,0:T(8,128)(2,1)}), (bf16[2560,640]{1,0:T(8,128)(2,1)}, bf16[2560,128]{1,0:T(8,128)(2,1)}, bf16[2560,128]{1,0:T(8,128)(2,1)})) %all-reduce.11.cloned.1.call-update) | async-done | bytes 4587536 | tf_op jit(solution)/shard_map/psum | solution.py:205
  555.5 5.3 convert_element_type.283
  (181 shorter events, 35.1 us)
Async XLA Ops:
  7.2 144.2 %copy-start = (bf16[16,128,128]{2,1,0:T(8,128)(2,1)S(1)}, bf16[16,128,128]{2,1,0:T(8,128)(2,1)}, u32[]{:S(2)}) copy-start(bf16[16,128,128]{2,1,0:T(8,128)(2,1)} %param.20) | copy-start | bytes 1572868
  7.2 29.3 %copy-start.22 = (f32[5120]{0:T(1024)S(1)}, f32[5120]{0:T(1024)}, u32[]{:S(2)}) copy-start(f32[5120]{0:T(1024)} %param.15) | copy-start | bytes 61444
  7.2 29.3 %all-gather.9.cloned.1.call-start = ((), (), s32[]{:S(2)}) async-start(), calls=%async_computation.3 | async-start | bytes 1966080 | tf_op jit(solution)/shard_map/all_gather | solution.py:103
  7.9 54.4 %all-gather.11.cloned.1.call-start = ((), (), s32[]{:S(2)}) async-start(), calls=%async_computation.4 | async-start | bytes 1966080 | tf_op jit(solution)/shard_map/all_gather | solution.py:104
  8.7 138.5 %all-gather.7.cloned.1.call-start = ((), (), s32[]{:S(2)}) async-start(), calls=%async_computation.2 | async-start | bytes 9830400 | tf_op jit(solution)/shard_map/all_gather | solution.py:102
  9.4 179.9 %all-reduce.7.cloned.1.call-start = ((), (), s32[]{:S(2)}) async-start(), calls=%async_computation.5 | async-start | bytes 327680 | tf_op jit(solution)/shard_map/psum | solution.py:129
  152.7 5.2 copy-start.30
  152.7 5.7 copy-start.34
  157.2 57.7 %all-gather.13.cloned.1.call-start = ((), (), s32[]{:S(2)}) async-start(), calls=%async_computation.7 | async-start | bytes 1966080 | tf_op jit(solution)/shard_map/all_gather | solution.py:149
  157.8 91.8 %all-reduce.9.cloned.1.call-start = ((), (), s32[]{:S(2)}) async-start(), calls=%async_computation.6 | async-start | bytes 327680 | tf_op jit(solution)/shard_map/psum | solution.py:129
  158.3 31.0 %copy-start.32 = (s32[16]{0:T(128)}, s32[16]{0:T(128)S(1)}, u32[]{:S(2)}) copy-start(s32[16]{0:T(128)S(1)} %select_reduce_fusion.1) | copy-start | bytes 196
  191.4 6.4 %copy-start.3 = (bf16[5120,128]{1,0:T(8,128)(2,1)S(1)}, bf16[5120,128]{1,0:T(8,128)(2,1)}, u32[]{:S(2)}) copy-start(bf16[5120,128]{1,0:T(8,128)(2,1)} %all-gather.9.cloned.1.call-done) | copy-start | bytes 3932164
  200.7 49.0 %copy-start.13 = (bf16[16,5120]{1,0:T(8,128)(2,1)S(1)}, bf16[16,5120]{1,0:T(8,128)(2,1)}, u32[]{:S(2)}) copy-start(bf16[16,5120]{1,0:T(8,128)(2,1)} %all-reduce.7.cloned.1.call-done) | copy-start | bytes 491524
  200.7 49.0 %copy-start.29 = (f32[5120]{0:T(1024)S(1)}, f32[5120]{0:T(1024)}, u32[]{:S(2)}) copy-start(f32[5120]{0:T(1024)} %param.23) | copy-start | bytes 61444
  205.2 61.8 %copy-start.33 = (s32[16]{0:T(128)S(1)}, s32[16]{0:T(128)}, u32[]{:S(2)}) copy-start(s32[16]{0:T(128)} %copy-done.32) | copy-start | bytes 196
  205.3 63.9 %copy-start.2 = (s32[32]{0:T(128)S(1)}, s32[32]{0:T(128)}, u32[]{:S(2)}) copy-start(s32[32]{0:T(128)} %param.24) | copy-start | bytes 388
  205.3 88.6 %all-gather.15.cloned.1.call-start = ((), (), s32[]{:S(2)}) async-start(), calls=%async_computation.8 | async-start | bytes 3276800 | tf_op jit(solution)/shard_map/all_gather | solution.py:159
  216.9 79.5 %copy-start.8 = (bf16[16,16,1280]{2,1,0:T(8,128)(2,1)}, bf16[16,16,1280]{2,1,0:T(8,128)(2,1)S(1)}, u32[]{:S(2)}) copy-start(bf16[16,16,1280]{2,1,0:T(8,128)(2,1)S(1)} %gather_fusion) | copy-start | bytes 1966084
  268.2 52.8 %all-gather.17.cloned.1.call-start = ((), (), s32[]{:S(2)}) async-start(), calls=%async_computation.10 | async-start | bytes 3276800 | tf_op jit(solution)/shard_map/all_gather | solution.py:160
  269.0 119.5 %reduce-scatter.2.cloned.1.call-start = ((), (), s32[]{:S(2)}) async-start(), calls=%async_computation.9 | async-start | bytes 3276800 | tf_op jit(solution)/shard_map/reduce_scatter | solution.py:172
  270.2 35.1 %copy-start.27 = (pred[16,16,16]{1,2,0:T(8,128)(4,1)}, pred[16,16,16]{1,2,0:T(8,128)(4,1)S(1)}, u32[]{:S(2)}) copy-start(pred[16,16,16]{1,2,0:T(8,128)(4,1)S(1)} %broadcast_and_fusion) | copy-start | bytes 12292
  302.7 4.4 copy-start.20
  327.3 6.2 %copy-start.14 = (bf16[16,16,1,5,128]{4,3,1,0,2:T(8,128)(2,1)}, bf16[16,16,1,5,128]{4,3,1,0,2:T(8,128)(2,1)S(1)}, u32[]{:S(2)}) copy-start(bf16[16,16,1,5,128]{4,3,1,0,2:T(8,128)(2,1)S(1)} %reshape.465) | copy-start | bytes 983044
  329.0 4.5 copy-start.26
  329.0 6.4 %copy-start.24 = (bf16[256,128]{1,0:T(8,128)(2,1)S(1)}, bf16[256,128]{1,0:T(8,128)(2,1)}, u32[]{:S(2)}) copy-start(bf16[256,128]{1,0:T(8,128)(2,1)} %copy-done.23) | copy-start | bytes 196612
  329.0 6.4 %copy-start.28 = (pred[16,16,16]{1,2,0:T(8,128)(4,1)S(1)}, pred[16,16,16]{1,2,0:T(8,128)(4,1)}, u32[]{:S(2)}) copy-start(pred[16,16,16]{1,2,0:T(8,128)(4,1)} %copy-done.27) | copy-start | bytes 12292
  329.0 50.6 %all-to-all-start = ((bf16[256,2,2560]{2,0,1:T(8,128)(2,1)}), bf16[256,2,2560]{2,0,1:T(8,128)(2,1)S(1)}, u32[]{:S(2)}, u32[]{:S(2)}) async-start(bf16[256,2,2560]{2,0,1:T(8,128)(2,1)} %bitcast.181), calls=%async_computation.1 | async-start | bytes 5242880 | tf_op jit(solution)/shard_map/all_to_all | solution.py:182
  333.2 222.3 %all-reduce.11.cloned.1.call-start = ((), (), s32[]{:S(2)}) async-start(), calls=%async_computation.11 | async-start | bytes 9175040 | tf_op jit(solution)/shard_map/psum | solution.py:205
  337.0 28.7 %copy-start.15 = (bf16[16,16,1,5,128]{4,3,1,0,2:T(8,128)(2,1)S(1)}, bf16[16,16,1,5,128]{4,3,1,0,2:T(8,128)(2,1)}, u32[]{:S(2)}) copy-start(bf16[16,16,1,5,128]{4,3,1,0,2:T(8,128)(2,1)} %copy-done.14) | copy-start | bytes 983044
  555.5 5.3 copy-start.19
  555.5 6.4 %copy-start.18 = (bf16[2560,128]{1,0:T(8,128)(2,1)S(1)}, bf16[2560,128]{1,0:T(8,128)(2,1)}, u32[]{:S(2)}) copy-start(bf16[2560,128]{1,0:T(8,128)(2,1)} %get-tuple-element.12) | copy-start | bytes 1966084
  555.5 7.6 %copy-start.1 = (bf16[16,128,128]{2,1,0:T(8,128)(2,1)S(1)}, bf16[16,128,128]{2,1,0:T(8,128)(2,1)}, u32[]{:S(2)}) copy-start(bf16[16,128,128]{2,1,0:T(8,128)(2,1)} %param.20) | copy-start | bytes 1572868
  (14 other events, 29.0 us)
Sparse Core Ops, SparseCore 0:
  9.6 26.9 all-gather.8
  38.1 24.2 all-gather.10
  63.9 83.2 all-gather.6
  157.4 31.9 all-reduce.6
  190.7 24.2 all-gather.12
  217.7 31.9 all-reduce.8
  268.3 25.5 all-gather.14
  295.5 25.5 all-gather.16
  323.6 34.3 reduce-scatter.1
  388.6 166.8 all-reduce.10
where the time goes:
time: 571 us; the launch traced here: 570 us
  waiting for transfers between devices  404 us (71%)
  matrix products  54.5 us (10%)
  blocking collectives  52.2 us (9%)
  other arithmetic  24.9 us (4%)
  between operations  18.2 us (3%)
  local copies, waits for them, and re-layouts  11 us (2%)
    psum x1, waiting for transfers between devices, on_device(): lax.psum(shard_q.astype(jnp.bfloat16), 'grp').astype(jnp.float32)  164 us
    all_gather x1, waiting for transfers between devices, on_device(): lax.all_gather(w_query, 'dp', axis=0, tiled=True)  83.2 us
    psum x2, waiting for transfers between devices, on_device(): lax.psum(partial_out.astype(jnp.bfloat16), 'tp').astype(jnp.float32)  62.5 us
    all_gather x1, blocking collectives, on_device(): lax.all_gather(d_key, 'dp', axis=0, tiled=True)  28.2 us
    all_gather x1, waiting for transfers between devices, on_device(): lax.all_gather(w_key, 'dp', axis=0, tiled=True)  26.9 us
    all_gather x1, waiting for transfers between devices, on_device(): lax.all_gather(w_value, 'dp', axis=0, tiled=True)  24.2 us
    all_gather x1, waiting for transfers between devices, on_device(): lax.all_gather(local_in, 'tp', axis=1, tiled=True)  23.7 us
    dot_general x3, matrix products, on_device(): partial_out = jnp.dot(context, w_out, preferred_element_type=jnp.float32)  15.7 us
  transfers between devices with their start and end apart: 11, of which 9 were waited for; matrix products, arithmetic and copies ran while one was open for 12% of the time, Pallas kernels for 0%

commit v1 on v0

--- a/solution.py
+++ b/solution.py
@@ -5,6 +5,12 @@
 
 HEAD_DIM = 128
 STEPS = 2
+
+
+def add_all(shard, name):
+    shards = lax.all_gather(shard, name, axis=0, tiled=False)
+    total = shards.sum(axis=0)
+    return total
 
 
 def norm_rows(values, gain):
@@ -202,7 +208,7 @@
             totals[which] = totals[which] + rounded(term)
     shard_q, shard_k, shard_v = tuple(totals)
     grad_q, grad_k, grad_v = (
-        lax.psum(shard_q.astype(jnp.bfloat16), "grp").astype(jnp.float32),
+        add_all(shard_q.astype(jnp.bfloat16), "grp").astype(jnp.float32),
         lax.psum(shard_k.astype(jnp.bfloat16), "grp").astype(jnp.float32),
         lax.psum(shard_v.astype(jnp.bfloat16), "grp").astype(jnp.float32),
     )

time: 571 us -> 708 us (1.24)
  waiting for transfers between devices: 404 us -> 532 us
  other arithmetic: 24.9 us -> 36.1 us
    all_gather x0 -> x1, waiting for transfers between devices: none -> 227 us  [add_all(): shards = lax.all_gather(shard, name, axis=0, tiled=False)]
    psum x1, waiting for transfers between devices: 164 us -> 35.1 us  [on_device(): lax.psum(shard_k.astype(jnp.bfloat16), 'grp').astype(jnp.float32)]
    reduce_scatter x1, waiting for transfers between devices: 0.02 us -> 31.9 us  [on_device(): lax.psum_scatter(partial_out.astype(jnp.bfloat16), 'tp', scatter_dimensio...]
    all_gather x1, blocking collectives: 28.2 us -> 4.94 us  [on_device(): lax.all_gather(d_key, 'dp', axis=0, tiled=True)]
    all_gather x1, blocking collectives: 4.94 us -> 21.1 us  [on_device(): lax.all_gather(d_value, 'dp', axis=0, tiled=True)]
    reduce_sum x0 -> x1, other arithmetic: none -> 9.24 us  [add_all(): total = shards.sum(axis=0)]
    dot_general x6, matrix products: 4.68 us -> 12.6 us  [on_device(): lax.dot_general(left, right, (((0,), (0,)), ((), ())), preferred_element_...]
  transfers between devices with their start and end apart: 11 -> 12, of which waited for: 9 -> 11; matrix products, arithmetic and copies ran while one was open for 12% -> 10% of each run, Pallas kernels for 0% -> 0%
where the time goes in v1:
time: 708 us; the launch traced here: 707 us
  waiting for transfers between devices  532 us (75%)
  matrix products  59.7 us (8%)
  blocking collectives  45.3 us (6%)
  other arithmetic  36.1 us (5%)
  between operations  17.7 us (2%)
  local copies, waits for them, and re-layouts  10.7 us (2%)
    all_gather x1, waiting for transfers between devices, add_all(): shards = lax.all_gather(shard, name, axis=0, tiled=False)  227 us
    all_gather x1, waiting for transfers between devices, on_device(): lax.all_gather(w_query, 'dp', axis=0, tiled=True)  83.2 us
    psum x2, waiting for transfers between devices, on_device(): lax.psum(partial_out.astype(jnp.bfloat16), 'tp').astype(jnp.float32)  64.2 us
    psum x1, waiting for transfers between devices, on_device(): lax.psum(shard_k.astype(jnp.bfloat16), 'grp').astype(jnp.float32)  35.1 us
    reduce_scatter x1, waiting for transfers between devices, on_device(): lax.psum_scatter(partial_out.astype(jnp.bfloat16), 'tp', scatter_dimensio...  31.9 us
    all_gather x1, waiting for transfers between devices, on_device(): lax.all_gather(w_key, 'dp', axis=0, tiled=True)  26.9 us
    all_gather x1, waiting for transfers between devices, on_device(): lax.all_gather(w_value, 'dp', axis=0, tiled=True)  24.2 us
    all_gather x1, waiting for transfers between devices, on_device(): lax.all_gather(local_in, 'tp', axis=1, tiled=True)  21.2 us
  transfers between devices with their start and end apart: 12, of which 11 were waited for; matrix products, arithmetic and copies ran while one was open for 10% of the time, Pallas kernels for 0%

profile of v1, /device:TPU:0, one launch (start us, length us, event | category | flops | bytes accessed | tf_op | source)
XLA Modules:
  0.0 706.9 jit_solution(10655818466756849814)
XLA Ops:
  9.7 26.9 %all-gather.11.cloned.1.call-done = bf16[5120,128]{1,0:T(8,128)(2,1)} async-done(((bf16[2560,128]{1,0:T(8,128)(2,1)}), bf16[5120,128]{1,0:T(8,128)(2,1)}) %all-gather.11.cloned.1.call-update) | async-done | bytes 1310736 | tf_op jit(solution)/shard_map/all_gather | solution.py:109
  38.2 24.2 %all-gather.13.cloned.1.call-done = bf16[5120,128]{1,0:T(8,128)(2,1)} async-done(((bf16[2560,128]{1,0:T(8,128)(2,1)}), bf16[5120,128]{1,0:T(8,128)(2,1)}) %all-gather.13.cloned.1.call-update) | async-done | bytes 1310736 | tf_op jit(solution)/shard_map/all_gather | solution.py:110
  64.0 83.2 %all-gather.9.cloned.1.call-done = bf16[5120,640]{1,0:T(8,128)(2,1)} async-done(((bf16[2560,640]{1,0:T(8,128)(2,1)}), bf16[5120,640]{1,0:T(8,128)(2,1)}) %all-gather.9.cloned.1.call-update) | async-done | bytes 6553616 | tf_op jit(solution)/shard_map/all_gather | solution.py:108
  147.2 3.8 convolution_convert_fusion.16
  152.7 4.5 convolution_convert_fusion.2
  157.8 31.4 %all-reduce.7.cloned.1.call-done = bf16[16,5120]{1,0:T(8,128)(2,1)} async-done(((bf16[16,5120]{1,0:T(8,128)(2,1)}), bf16[16,5120]{1,0:T(8,128)(2,1)}) %all-reduce.7.cloned.1.call-update) | async-done | bytes 163856 | tf_op jit(solution)/shard_map/psum | solution.py:135
  191.4 4.5 convolution_convert_fusion.15
  200.7 4.5 convolution_convert_fusion.1
  207.8 7.1 %all-gather.15.cloned.1.call-done = bf16[32,16,1280]{2,1,0:T(8,128)(2,1)} async-done(((bf16[16,16,1280]{2,1,0:T(8,128)(2,1)}), bf16[32,16,1280]{2,1,0:T(8,128)(2,1)}) %all-gather.15.cloned.1.call-update) | async-done | bytes 1310736 | tf_op jit(solution)/shard_map/all_gather | solution.py:155
  216.8 32.8 %all-reduce.9.cloned.1.call-done = bf16[16,5120]{1,0:T(8,128)(2,1)} async-done(((bf16[16,5120]{1,0:T(8,128)(2,1)}), bf16[16,5120]{1,0:T(8,128)(2,1)}) %all-reduce.9.cloned.1.call-update) | async-done | bytes 163856 | tf_op jit(solution)/shard_map/psum | solution.py:135
  249.6 2.3 fusion.36
  252.5 5.5 all-reduce.1
  261.4 4.9 all-reduce
  269.0 7.7 %all-gather.19.cloned.1.call-done = bf16[256,5120]{1,0:T(8,128)(2,1)} async-done(((bf16[256,1280]{1,0:T(8,128)(2,1)}), bf16[256,5120]{1,0:T(8,128)(2,1)}) %all-gather.19.cloned.1.call-update) | async-done | bytes 2621456 | tf_op jit(solution)/shard_map/all_gather | solution.py:166
  276.8 5.9 fusion.6
  283.2 21.2 %all-gather.17.cloned.1.call-done = bf16[256,5120]{1,0:T(8,128)(2,1)} async-done(((bf16[256,1280]{1,0:T(8,128)(2,1)}), bf16[256,5120]{1,0:T(8,128)(2,1)}) %all-gather.17.cloned.1.call-update) | async-done | bytes 2621456 | tf_op jit(solution)/shard_map/all_gather | solution.py:165
  304.5 2.5 fusion
  309.4 5.2 all-to-all-start
  314.7 5.1 convolution_convert_fusion.11
  320.9 2.3 convolution_convert_fusion.13
  326.0 21.1 %all_gather.47 = bf16[512,128]{1,0:T(8,128)(2,1)S(1)} all-gather(bf16[256,128]{1,0:T(8,128)(2,1)S(1)} %bitcast.191), channel_id=1, replica_groups=mesh['grp'=4,'dp'=2,'tp'=4] {'dp'}, dimensions={0}, use_global_device_ids=true | all-gather | bytes 196608 | tf_op jit(solution)/shard_map/all_gather | solution.py:196
  347.5 4.9 all_gather.46
  361.9 6.5 convolution_convert_fusion
  369.0 8.8 %all_gather.43 = bf16[512,640]{1,0:T(8,128)(2,1)S(1)} all-gather(bf16[256,640]{1,0:T(8,128)(2,1)S(1)} %bitcast.181), channel_id=1, replica_groups=mesh['grp'=4,'dp'=2,'tp'=4] {'dp'}, dimensions={0}, use_global_device_ids=true | all-gather | bytes 983040 | tf_op jit(solution)/shard_map/all_gather | solution.py:194
  377.9 2.5 convolution_convert_fusion.4
  380.4 2.6 convolution_convert_fusion.3
  383.0 2.6 add_convert_fusion
  385.6 35.1 %all-reduce.11.cloned.1.call-done = (bf16[2560,128]{1,0:T(8,128)(2,1)}, bf16[2560,128]{1,0:T(8,128)(2,1)}) async-done(((bf16[2560,128]{1,0:T(8,128)(2,1)}, bf16[2560,128]{1,0:T(8,128)(2,1)}), (bf16[2560,128]{1,0:T(8,128)(2,1)}, bf16[2560,128]{1,0:T(8,128)(2,1)})) %all-reduce.11.cloned.1.call-update) | async-done | bytes 1310736 | tf_op jit(solution)/shard_map/psum | solution.py:212
  425.2 31.9 %reduce-scatter.2.cloned.1.call-done = bf16[256,1280]{1,0:T(8,128)(2,1)} async-done(((bf16[256,5120]{1,0:T(8,128)(2,1)}), bf16[256,1280]{1,0:T(8,128)(2,1)}) %reduce-scatter.2.cloned.1.call-update) | async-done | bytes 655376 | tf_op jit(solution)/shard_map/reduce_scatter | solution.py:178
  459.3 226.7 %all-gather.21.cloned.1.call-done = bf16[10240,640]{1,0:T(8,128)(2,1)} async-done(((bf16[2560,640]{1,0:T(8,128)(2,1)}), bf16[10240,640]{1,0:T(8,128)(2,1)}) %all-gather.21.cloned.1.call-update) | async-done | bytes 13107216 | tf_op jit(solution)/shard_map/all_gather | solution.py:11
  686.0 9.2 %reduce_sum.139 = bf16[2560,640]{1,0:T(8,128)(2,1)} reduce(bf16[4,2560,640]{2,1,0:T(8,128)(2,1)} %bitcast.176, bf16[]{:T(256)} %constant.84.clone.1), dimensions={0}, to_apply=%region_18.19 | reduce | flops 4915200 | bytes 16384002 | tf_op jit(solution)/shard_map/reduce_sum | solution.py:12
  695.2 5.1 convert_element_type.285
  (157 shorter events, 46.3 us)
Async XLA Ops:
  7.2 144.2 %copy-start = (bf16[16,128,128]{2,1,0:T(8,128)(2,1)S(1)}, bf16[16,128,128]{2,1,0:T(8,128)(2,1)}, u32[]{:S(2)}) copy-start(bf16[16,128,128]{2,1,0:T(8,128)(2,1)} %param.20) | copy-start | bytes 1572868
  7.2 2.3 copy-start.7
  7.2 2.5 copy-start.19
  7.2 29.3 %copy-start.16 = (f32[5120]{0:T(1024)S(1)}, f32[5120]{0:T(1024)}, u32[]{:S(2)}) copy-start(f32[5120]{0:T(1024)} %param.15) | copy-start | bytes 61444
  7.2 29.3 %all-gather.11.cloned.1.call-start = ((), (), s32[]{:S(2)}) async-start(), calls=%async_computation.3 | async-start | bytes 1966080 | tf_op jit(solution)/shard_map/all_gather | solution.py:109
  7.9 54.4 %all-gather.13.cloned.1.call-start = ((), (), s32[]{:S(2)}) async-start(), calls=%async_computation.4 | async-start | bytes 1966080 | tf_op jit(solution)/shard_map/all_gather | solution.py:110
  8.7 138.5 %all-gather.9.cloned.1.call-start = ((), (), s32[]{:S(2)}) async-start(), calls=%async_computation.2 | async-start | bytes 9830400 | tf_op jit(solution)/shard_map/all_gather | solution.py:108
  9.4 179.8 %all-reduce.7.cloned.1.call-start = ((), (), s32[]{:S(2)}) async-start(), calls=%async_computation.5 | async-start | bytes 327680 | tf_op jit(solution)/shard_map/psum | solution.py:135
  157.2 57.7 %all-gather.15.cloned.1.call-start = ((), (), s32[]{:S(2)}) async-start(), calls=%async_computation.7 | async-start | bytes 1966080 | tf_op jit(solution)/shard_map/all_gather | solution.py:155
  157.8 91.8 %all-reduce.9.cloned.1.call-start = ((), (), s32[]{:S(2)}) async-start(), calls=%async_computation.6 | async-start | bytes 327680 | tf_op jit(solution)/shard_map/psum | solution.py:135
  191.4 6.4 copy-start.3
  195.9 4.0 copy-start.4
  198.1 2.1 copy-start.11
  200.7 5.4 copy-start.20
  200.7 6.7 copy-start.18
  200.7 48.9 %copy-start.12 = (bf16[16,5120]{1,0:T(8,128)(2,1)S(1)}, bf16[16,5120]{1,0:T(8,128)(2,1)}, u32[]{:S(2)}) copy-start(bf16[16,5120]{1,0:T(8,128)(2,1)} %all-reduce.7.cloned.1.call-done) | copy-start | bytes 491524
  200.7 48.9 %copy-start.17 = (f32[5120]{0:T(1024)S(1)}, f32[5120]{0:T(1024)}, u32[]{:S(2)}) copy-start(f32[5120]{0:T(1024)} %param.23) | copy-start | bytes 61444
  205.3 71.5 %all-gather.19.cloned.1.call-start = ((), (), s32[]{:S(2)}) async-start(), calls=%async_computation.10 | async-start | bytes 3276800 | tf_op jit(solution)/shard_map/all_gather | solution.py:166
  205.3 62.9 %copy-start.2 = (s32[32]{0:T(128)S(1)}, s32[32]{0:T(128)}, u32[]{:S(2)}) copy-start(s32[32]{0:T(128)} %param.24) | copy-start | bytes 388
  206.0 98.4 %all-gather.17.cloned.1.call-start = ((), (), s32[]{:S(2)}) async-start(), calls=%async_computation.8 | async-start | bytes 3276800 | tf_op jit(solution)/shard_map/all_gather | solution.py:165
  216.8 65.8 %copy-start.8 = (bf16[16,16,1280]{2,1,0:T(8,128)(2,1)}, bf16[16,16,1280]{2,1,0:T(8,128)(2,1)S(1)}, u32[]{:S(2)}) copy-start(bf16[16,16,1280]{2,1,0:T(8,128)(2,1)S(1)} %gather_fusion) | copy-start | bytes 1966084
  304.5 2.5 copy-start.6
  309.4 43.0 %all-to-all-start = ((bf16[256,2,2560]{2,0,1:T(8,128)(2,1)}), bf16[256,2,2560]{2,0,1:T(8,128)(2,1)}, u32[]{:S(2)}, u32[]{:S(2)}) async-start(bf16[256,2,2560]{2,0,1:T(8,128)(2,1)} %bitcast.177), calls=%async_computation.1 | async-start | bytes 5242880 | tf_op jit(solution)/shard_map/all_to_all | solution.py:188
  314.6 106.1 %all-reduce.11.cloned.1.call-start = ((), (), s32[]{:S(2)}) async-start(), calls=%async_computation.12 | async-start | bytes 2621440 | tf_op jit(solution)/shard_map/psum | solution.py:212
  320.9 2.3 copy-start.15
  320.9 3.1 copy-start.5
  324.0 23.1 %copy-start.13 = (f32[16,1,5,16,16]{3,4,2,0,1:T(8,128)}, f32[16,1,5,16,16]{3,4,2,0,1:T(8,128)S(1)}, u32[]{:S(2)}) copy-start(f32[16,1,5,16,16]{3,4,2,0,1:T(8,128)S(1)} %get-tuple-element.20) | copy-start | bytes 245764
  359.9 1.5 copy-start.14
  361.4 95.7 %reduce-scatter.2.cloned.1.call-start = ((), (), s32[]{:S(2)}) async-start(), calls=%async_computation.9 | async-start | bytes 3276800 | tf_op jit(solution)/shard_map/reduce_scatter | solution.py:178
  368.4 317.6 %all-gather.21.cloned.1.call-start = ((), (), s32[]{:S(2)}) async-start(), calls=%async_computation.11 | async-start | bytes 16384000 | tf_op jit(solution)/shard_map/all_gather | solution.py:11
  385.6 71.5 %copy-start.9 = (bf16[16,16,1280]{2,1,0:T(8,128)(2,1)S(1)}, bf16[16,16,1280]{2,1,0:T(8,128)(2,1)}, u32[]{:S(2)}) copy-start(bf16[16,16,1280]{2,1,0:T(8,128)(2,1)} %copy-done.8) | copy-start | bytes 1966084
  686.0 14.4 %copy-start.1 = (bf16[16,128,128]{2,1,0:T(8,128)(2,1)S(1)}, bf16[16,128,128]{2,1,0:T(8,128)(2,1)}, u32[]{:S(2)}) copy-start(bf16[16,128,128]{2,1,0:T(8,128)(2,1)} %param.20) | copy-start | bytes 1572868
  (1 other events, 1.3 us)
Sparse Core Ops, SparseCore 0:
  9.6 26.9 all-gather.10
  38.1 24.2 all-gather.12
  63.9 83.2 all-gather.8
  157.3 31.9 all-reduce.6
  190.7 24.2 all-gather.14
  217.7 31.9 all-reduce.8
  251.2 25.5 all-gather.18
  278.9 25.5 all-gather.16
  361.5 59.1 all-reduce.10
  423.1 33.9 reduce-scatter.1
  459.2 226.7 all-gather.20
